TPU v7x, 32 devices: a whole 2x2x4 slice. The times are simulated.
32 devices in a mesh: cand: 4 (over y, core), tensor: 8 (over z, x).
Axes of the slice: x: 2, y: 2, z: 4, core: 2. Of those that a mesh axis runs over, the one named last changes fastest.
Arguments:
- states: bfloat16 [512, 3584], P('cand'), may hold values from -60 to 60
- targets: int32 [512], replicated, may hold values from 0 to 131071
- loss_mask: int32 [512], P('cand'), may hold values 0 or 1
- cand_of: int32 [4], replicated, may hold values from 0 to 3
- lambdas: float32 [4], replicated, may hold values from 0.2 to 1
- base_q: bfloat16 [3584, 4096], P('cand', 'tensor'), may hold values from -0.09375 to 0.09375
- delta_q: bfloat16 [2, 3584, 4096], P(None, 'cand', 'tensor'), may hold values from -0.046875 to 0.046875
- base_k: bfloat16 [3584, 2048], P('cand'), may hold values from -0.09375 to 0.09375
- delta_k: bfloat16 [2, 3584, 2048], P(None, 'cand'), may hold values from -0.046875 to 0.046875
- base_v: bfloat16 [3584, 2048], P('cand'), may hold values from -0.09375 to 0.09375
- delta_v: bfloat16 [2, 3584, 2048], P(None, 'cand'), may hold values from -0.046875 to 0.046875
- base_o: bfloat16 [4096, 3584], P('tensor', 'cand'), may hold values from -0.09375 to 0.09375
- delta_o: bfloat16 [2, 4096, 3584], P(None, 'tensor', 'cand'), may hold values from -0.046875 to 0.046875
- pre_gain: float32 [3584], replicated, may hold values from 0.5 to 2
- post_gain: float32 [3584], replicated, may hold values from 0.5 to 2
- final_gain: float32 [3584], replicated, may hold values from 0.5 to 2
- unembed: bfloat16 [3584, 131072], P(None, ('cand', 'tensor')), may hold values from -0.3125 to 0.3125
Outputs:
- token_loss: float32 [512], P('cand')
- cand_loss: float32 [4], replicated
All inputs are finite; a program needn't handle non-finite values. No bound on the sum of `loss_mask` on one device may be relied on, other than what follows from the above.
Results may differ from a plain program's by a relative error of at most 0.002.
Values may be sent and summed in bfloat16 or wider, within the bound.
No kernel may reach another device: no remote copies, remote signals or barrier semaphores. Data moves between devices by JAX's collectives and lax.ppermute only.
A program may use at most 128 MiB of HBM per device.

v0:
```python
import math
import jax
import jax.numpy as jnp
from jax import lax
from jax.sharding import PartitionSpec as P

KV = 8
HEAD_SIZE = 256
CANDS = 4


def root_norm(entries, scale_gain):
    mean_square = jnp.mean(entries * entries, axis=-1, keepdims=True)
    return entries * lax.rsqrt(mean_square + 1e-06) * scale_gain


def rotate_pairs(entries, length):
    half_width = entries.shape[-1] // 2
    positions = jnp.arange(length).astype(jnp.float32)
    frequency = jnp.exp(
        -math.log(10000.0) * jnp.arange(half_width).astype(jnp.float32) * 2.0 / entries.shape[-1]
    )
    angles = positions[:, None] * frequency[None, :]
    cosine = jnp.cos(angles)[:, None, :]
    sine_part = jnp.sin(angles)[:, None, :]
    first = entries[..., :half_width]
    second = entries[..., half_width:]
    return jnp.concatenate(
        [first * cosine - second * sine_part, second * cosine + first * sine_part], axis=-1
    )


def task_total(delta):
    return jnp.sum(delta.astype(jnp.float32), axis=0).astype(jnp.bfloat16)


def merge_weights(base, total, mixing):
    return (base.astype(jnp.float32) + mixing * total.astype(jnp.float32)).astype(jnp.bfloat16)


def on_device(
    states,
    targets,
    loss_mask,
    cand_of,
    lambdas,
    base_q,
    delta_q,
    base_k,
    delta_k,
    base_v,
    delta_v,
    base_o,
    delta_o,
    pre_gain,
    post_gain,
    final_gain,
    unembed,
):
    cand_id = lax.axis_index("cand")
    tensor_id = lax.axis_index("tensor")
    tensor_count = lax.axis_size("tensor")
    chosen = cand_of[cand_id]
    mixing = lambdas[chosen]
    group_size = tensor_count // KV
    head_start = tensor_id // group_size * HEAD_SIZE
    own_base_k = lax.dynamic_slice_in_dim(base_k, head_start, HEAD_SIZE, 1)
    own_base_v = lax.dynamic_slice_in_dim(base_v, head_start, HEAD_SIZE, 1)
    own_delta_k = lax.dynamic_slice_in_dim(delta_k, head_start, HEAD_SIZE, 2)
    own_delta_v = lax.dynamic_slice_in_dim(delta_v, head_start, HEAD_SIZE, 2)
    summed = [task_total(delta) for delta in (delta_q, own_delta_k, own_delta_v, delta_o)]
    pieces = (
        lax.all_gather(base_q, "cand", axis=0, tiled=True),
        lax.all_gather(own_base_k, "cand", axis=0, tiled=True),
        lax.all_gather(own_base_v, "cand", axis=0, tiled=True),
        lax.all_gather(base_o, "cand", axis=1, tiled=True),
        lax.all_gather(summed[0], "cand", axis=0, tiled=True),
        lax.all_gather(summed[1], "cand", axis=0, tiled=True),
        lax.all_gather(summed[2], "cand", axis=0, tiled=True),
        lax.all_gather(summed[3], "cand", axis=1, tiled=True),
    )
    base_parts = pieces[:4]
    task_parts = pieces[4:]
    w_query = merge_weights(base_parts[0], task_parts[0], mixing)
    w_key = merge_weights(base_parts[1], task_parts[1], mixing)
    w_value = merge_weights(base_parts[2], task_parts[2], mixing)
    w_out = merge_weights(base_parts[3], task_parts[3], mixing)
    length = states.shape[0]
    stream = states.astype(jnp.float32)
    normed = root_norm(stream, pre_gain).astype(jnp.bfloat16)
    query_rows = jnp.dot(normed, w_query, preferred_element_type=jnp.float32).reshape(
        length, -1, HEAD_SIZE
    )
    query_rows = rotate_pairs(query_rows, length).astype(jnp.bfloat16)
    key_full = jnp.dot(normed, w_key, preferred_element_type=jnp.float32).astype(jnp.bfloat16)
    value_full = jnp.dot(normed, w_value, preferred_element_type=jnp.float32).astype(jnp.bfloat16)
    key_matrix = rotate_pairs(
        key_full.astype(jnp.float32).reshape(length, 1, HEAD_SIZE), length
    ).astype(jnp.bfloat16)[:, 0, :]
    attention_scores = jnp.einsum(
        "lhd,md->hlm", query_rows, key_matrix, preferred_element_type=jnp.float32
    ) * HEAD_SIZE ** (-0.5)
    attention_scores = 50.0 * jnp.tanh(attention_scores / 50.0)
    causal = jnp.arange(length)[:, None] >= jnp.arange(length)[None, :]
    weights = jnp.where(causal[None, :, :], jnp.exp(attention_scores), 0.0)
    attention_probs = (weights / jnp.sum(weights, axis=-1, keepdims=True)).astype(jnp.bfloat16)
    context_rows = jnp.einsum(
        "hlm,md->lhd", attention_probs, value_full, preferred_element_type=jnp.float32
    )
    context_rows = context_rows.astype(jnp.bfloat16).reshape(length, -1)
    partial_value = jnp.dot(context_rows, w_out, preferred_element_type=jnp.float32)
    vocab_width = unembed.shape[1]
    vocab_start = (cand_id * tensor_count + tensor_id) * vocab_width
    vocab_index = jnp.arange(vocab_width)
    attended = lax.psum(partial_value, "tensor")
    final_rows = root_norm(stream + root_norm(attended, post_gain), final_gain).astype(jnp.bfloat16)
    logits = jnp.dot(
        lax.all_gather(final_rows, "cand", axis=0, tiled=True),
        unembed,
        preferred_element_type=jnp.float32,
    )
    capped = 30.0 * jnp.tanh(logits / 30.0)
    totals = jnp.sum(jnp.exp(capped), axis=1)
    local_ids = targets - vocab_start
    matches = local_ids[:, None] == vocab_index[None, :]
    picked = jnp.sum(jnp.where(matches, capped, 0.0), axis=1)
    vocab_sums = jnp.stack([totals, picked], axis=0)
    summed_terms = lax.psum(vocab_sums, ("cand", "tensor"))
    own_terms = lax.dynamic_slice_in_dim(summed_terms, cand_id * length, length, 1)
    mask_values = loss_mask.astype(jnp.float32)
    token_loss = mask_values * (jnp.log(own_terms[0]) - own_terms[1])
    onehot = (chosen == jnp.arange(CANDS)).astype(jnp.float32)
    loss_sums, counts = lax.psum(
        (onehot * jnp.sum(token_loss), onehot * jnp.sum(mask_values)), "cand"
    )
    return (token_loss, loss_sums / jnp.maximum(counts, 1.0))


def solution(mesh):
    in_specs = (
        P("cand", None),
        P(),
        P("cand"),
        P(),
        P(),
        P("cand", "tensor"),
        P(None, "cand", "tensor"),
        P("cand", None),
        P(None, "cand", None),
        P("cand", None),
        P(None, "cand", None),
        P("tensor", "cand"),
        P(None, "tensor", "cand"),
        P(),
        P(),
        P(),
        P(None, ("cand", "tensor")),
    )
    out_specs = (P("cand"), P())
    return jax.shard_map(
        on_device, mesh=mesh, in_specs=in_specs, out_specs=out_specs, check_vma=False
    )
```

profile of v0, /device:TPU:0, one launch (start us, length us, event | category | flops | bytes accessed | tf_op | source)
XLA Modules:
  0.0 451.5 jit_solution(439209231556427896)
XLA Ops:
  7.2 0.0 copy-start.2
  7.2 0.0 all-gather.14.cloned.1.call-start
  7.2 1.9 constant_dynamic-slice_fusion.1
  9.2 0.0 all-gather.14.cloned.1.call-update
  9.2 0.0 all-gather.16.cloned.1.call-start
  9.2 2.3 dynamic-slice_reduce_fusion
  11.5 0.0 all-gather.16.cloned.1.call-update
  11.6 0.0 all-gather.20.cloned.1.call-start
  11.6 0.0 copy-done.2
  11.6 1.6 reduce_sum.123
  13.2 0.0 all-gather.20.cloned.1.call-update
  13.2 0.0 all-gather.18.cloned.1.call-start
  13.2 0.5 all-gather.18.cloned.1.call-update
  13.8 0.0 all-gather.10.cloned.1.call-start
  13.8 1.8 constant_dynamic-slice_fusion.2
  15.7 0.0 all-gather.10.cloned.1.call-update
  15.7 0.0 copy-start.8
  15.7 0.0 all-gather.12.cloned.1.call-start
  15.7 2.4 dynamic-slice_reduce_fusion.1
  18.1 0.0 all-gather.12.cloned.1.call-update
  18.2 0.0 all-gather.24.cloned.1.call-start
  18.2 1.5 reduce_sum.125
  19.7 0.0 all-gather.24.cloned.1.call-update
  19.7 0.0 all-gather.22.cloned.1.call-start
  19.8 0.7 all-gather.22.cloned.1.call-update
  20.5 0.0 all-reduce.3.cloned.1.call-start
  20.6 0.6 dynamic_slice.22
  23.1 0.6 dynamic_slice.23
  23.7 0.3 fusion.4
  24.0 0.3 multiply_cosine_fusion
  24.3 9.1 %all-gather.14.cloned.1.call-done = bf16[3584,256]{1,0:T(8,128)(2,1)} async-done(((bf16[896,256]{1,0:T(8,128)(2,1)}), bf16[3584,256]{1,0:T(8,128)(2,1)}) %all-gather.14.cloned.1.call-update) | async-done | bytes 1835024 | tf_op jit(solution)/shard_map/all_gather | solution.py:74
  33.4 22.7 %all-gather.16.cloned.1.call-done = bf16[3584,256]{1,0:T(8,128)(2,1)} async-done(((bf16[896,256]{1,0:T(8,128)(2,1)}), bf16[3584,256]{1,0:T(8,128)(2,1)}) %all-gather.16.cloned.1.call-update) | async-done | bytes 1835024 | tf_op jit(solution)/shard_map/all_gather | solution.py:78
  56.1 0.0 copy-done.8
  56.1 3.6 fusion.20
  59.7 0.3 fusion.37
  60.0 29.2 %all-gather.20.cloned.1.call-done = bf16[3584,512]{1,0:T(8,128)(2,1)} async-done(((bf16[896,512]{1,0:T(8,128)(2,1)}), bf16[3584,512]{1,0:T(8,128)(2,1)}) %all-gather.20.cloned.1.call-update) | async-done | bytes 3670032 | tf_op jit(solution)/shard_map/all_gather | solution.py:77
  89.2 32.9 %all-gather.18.cloned.1.call-done = bf16[3584,512]{1,0:T(8,128)(2,1)} async-done(((bf16[896,512]{1,0:T(8,128)(2,1)}), bf16[3584,512]{1,0:T(8,128)(2,1)}) %all-gather.18.cloned.1.call-update) | async-done | bytes 3670032 | tf_op jit(solution)/shard_map/all_gather | solution.py:73
  122.1 5.2 %fusion = f32[128,512]{1,0:T(8,128)S(1)} fusion(bf16[3584,512]{1,0:T(8,128)(2,1)} %all-gather.20.cloned.1.call-done, bf16[3584,512]{1,0:T(8,128)(2,1)} %all-gather.18.cloned.1.call-done, f32[]{:T(128)} %bitcast.1, bf16[128,3584]{1,0:T(8,128)(2,1)S(1)} %copy-done.1, f32[3584]{0:T(1024)S(1)} %copy-done.8, f32[128]{0:T(128)S(1)} %add_rsqrt_fusion.2), kind=kOutput, calls=%fused_computation.6 | convolution fusion | flops 480772096 | bytes 8534532 | tf_op jit(solution)/shard_map/dot_general | solution.py:91
  127.3 0.2 reshape.177
  127.5 0.1 fusion.53
  127.7 0.2 fusion.15
  127.9 16.7 %all-gather.10.cloned.1.call-done = bf16[3584,256]{1,0:T(8,128)(2,1)} async-done(((bf16[896,256]{1,0:T(8,128)(2,1)}), bf16[3584,256]{1,0:T(8,128)(2,1)}) %all-gather.10.cloned.1.call-update) | async-done | bytes 1835024 | tf_op jit(solution)/shard_map/all_gather | solution.py:75
  144.6 22.5 %all-gather.12.cloned.1.call-done = bf16[3584,256]{1,0:T(8,128)(2,1)} async-done(((bf16[896,256]{1,0:T(8,128)(2,1)}), bf16[3584,256]{1,0:T(8,128)(2,1)}) %all-gather.12.cloned.1.call-update) | async-done | bytes 1835024 | tf_op jit(solution)/shard_map/all_gather | solution.py:79
  167.2 3.9 convolution_convert_fusion
  171.1 29.1 %all-gather.24.cloned.1.call-done = bf16[512,3584]{1,0:T(8,128)(2,1)} async-done(((bf16[512,896]{1,0:T(8,128)(2,1)}), bf16[512,3584]{1,0:T(8,128)(2,1)}) %all-gather.24.cloned.1.call-update) | async-done | bytes 3670032 | tf_op jit(solution)/shard_map/all_gather | solution.py:80
  200.2 33.1 %all-gather.22.cloned.1.call-done = bf16[512,3584]{1,0:T(8,128)(2,1)} async-done(((bf16[512,896]{1,0:T(8,128)(2,1)}), bf16[512,3584]{1,0:T(8,128)(2,1)}) %all-gather.22.cloned.1.call-update) | async-done | bytes 3670032 | tf_op jit(solution)/shard_map/all_gather | solution.py:76
  233.3 6.6 %fusion.1 = f32[128,3584]{1,0:T(8,128)} fusion(bf16[128,512]{0,1:T(8,128)(2,1)S(1)} %bitcast.38, bf16[512,3584]{1,0:T(8,128)(2,1)} %all-gather.24.cloned.1.call-done, bf16[512,3584]{1,0:T(8,128)(2,1)} %all-gather.22.cloned.1.call-done, f32[]{:T(128)} %bitcast.1), kind=kOutput, calls=%fused_computation.7 | convolution fusion | flops 478937088 | bytes 9306116 | tf_op jit(solution)/shard_map/dot_general | solution.py:111
  239.9 0.0 all-reduce.3.cloned.1.call-update
  239.9 0.2 all-gather.26.cloned.1.call-start
  240.2 95.7 %all-reduce.3.cloned.1.call-done = f32[128,3584]{1,0:T(8,128)} async-done(((f32[128,3584]{1,0:T(8,128)}), f32[128,3584]{1,0:T(8,128)}) %all-reduce.3.cloned.1.call-update) | async-done | bytes 1835024 | tf_op jit(solution)/shard_map/psum | solution.py:115
  335.9 1.8 multiply_reduce_fusion.1
  337.8 0.0 copy-done.4
  337.8 0.0 copy-start.6
  337.8 2.0 multiply_reduce_fusion
  339.8 1.4 multiply_convert_fusion
  341.2 0.0 all-gather.26.cloned.1.call-update
  341.3 0.0 copy-start.7
  341.3 31.1 %all-gather.26.cloned.1.call-done = bf16[512,3584]{1,0:T(8,128)(2,1)} async-done(((bf16[128,3584]{1,0:T(8,128)(2,1)}), bf16[512,3584]{1,0:T(8,128)(2,1)}) %all-gather.26.cloned.1.call-update) | async-done | bytes 3670032 | tf_op jit(solution)/shard_map/all_gather | solution.py:118
  372.4 22.9 %exponential_reduce_fusion = (f32[512]{0:T(512)S(1)}, f32[512]{0:T(512)S(1)}) fusion(s32[512]{0:T(512)S(1)} %broadcast_subtract_fusion, bf16[512,3584]{1,0:T(8,128)(2,1)} %all-gather.26.cloned.1.call-done, bf16[3584,4096]{1,0:T(8,128)(2,1)} %param.33), kind=kOutput, calls=%fused_computation.2 | convolution fusion | flops 15044968448 | bytes 33036288 | tf_op jit(solution)/shard_map/dot_general | solution.py:117
  395.3 39.3 %psum.29 = f32[2,512]{1,0:T(2,128)S(1)} all-reduce(f32[2,512]{1,0:T(2,128)S(1)} %pad_maximum_fusion), channel_id=1, replica_groups=mesh['cand'=4,'tensor'=8] {'cand','tensor'}, use_global_device_ids=true, to_apply=%region_11.12 | all-reduce | flops 1024 | bytes 8192 | tf_op jit(solution)/shard_map/psum | solution.py:128
  434.7 1.1 fusion.52
  435.8 1.8 compare_select_fusion
  437.6 6.5 %all-reduce = (f32[4]{0:T(128)S(1)}, f32[4]{0:T(128)S(1)}) all-reduce(f32[4]{0:T(128)S(1)} %get-tuple-element.18, f32[4]{0:T(128)S(1)} %get-tuple-element.17), channel_id=1, replica_groups=mesh['cand'=4,'tensor'=8] {'cand'}, use_global_device_ids=true, to_apply=%region_13.14 | all-reduce | flops 8 | bytes 64 | tf_op jit(solution)/shard_map/psum | solution.py:133
  444.2 0.5 maximum_divide_fusion
  (25 shorter events, 0.1 us)
Async XLA Ops:
  7.2 4.4 copy-start.2
  7.2 26.2 %all-gather.14.cloned.1.call-start = ((), (), s32[]{:S(2)}) async-start(), calls=%async_computation.2 | async-start | bytes 2293760 | tf_op jit(solution)/shard_map/all_gather | solution.py:74
  9.2 46.9 %all-gather.16.cloned.1.call-start = ((), (), s32[]{:S(2)}) async-start(), calls=%async_computation.3 | async-start | bytes 2293760 | tf_op jit(solution)/shard_map/all_gather | solution.py:78
  11.6 77.6 %all-gather.20.cloned.1.call-start = ((), (), s32[]{:S(2)}) async-start(), calls=%async_computation.5 | async-start | bytes 4587520 | tf_op jit(solution)/shard_map/all_gather | solution.py:77
  13.2 5.0 %copy-start.3 = (bf16[2,512,896]{2,1,0:T(8,128)(2,1)S(1)}, bf16[2,512,896]{2,1,0:T(8,128)(2,1)}, u32[]{:S(2)}) copy-start(bf16[2,512,896]{2,1,0:T(8,128)(2,1)} %param.29) | copy-start | bytes 5505028
  13.2 108.9 %all-gather.18.cloned.1.call-start = ((), (), s32[]{:S(2)}) async-start(), calls=%async_computation.4 | async-start | bytes 4587520 | tf_op jit(solution)/shard_map/all_gather | solution.py:73
  13.8 130.9 %all-gather.10.cloned.1.call-start = ((), (), s32[]{:S(2)}) async-start(), calls=%async_computation | async-start | bytes 2293760 | tf_op jit(solution)/shard_map/all_gather | solution.py:75
  15.6 4.9 %copy-start.9 = (s32[4]{0:T(128)S(1)}, s32[4]{0:T(128)}, u32[]{:S(2)}) copy-start(s32[4]{0:T(128)} %param.20) | copy-start | bytes 52
  15.6 7.4 %copy-start.10 = (f32[4]{0:T(128)S(1)}, f32[4]{0:T(128)}, u32[]{:S(2)}) copy-start(f32[4]{0:T(128)} %param.21) | copy-start | bytes 52
  15.7 8.1 %copy-start.1 = (bf16[128,3584]{1,0:T(8,128)(2,1)S(1)}, bf16[128,3584]{1,0:T(8,128)(2,1)}, u32[]{:S(2)}) copy-start(bf16[128,3584]{1,0:T(8,128)(2,1)} %param.17) | copy-start | bytes 2752516
  15.7 40.4 %copy-start.8 = (f32[3584]{0:T(1024)S(1)}, f32[3584]{0:T(1024)}, u32[]{:S(2)}) copy-start(f32[3584]{0:T(1024)} %param.30) | copy-start | bytes 43012
  15.7 151.5 %all-gather.12.cloned.1.call-start = ((), (), s32[]{:S(2)}) async-start(), calls=%async_computation.1 | async-start | bytes 2293760 | tf_op jit(solution)/shard_map/all_gather | solution.py:79
  18.2 182.1 %all-gather.24.cloned.1.call-start = ((), (), s32[]{:S(2)}) async-start(), calls=%async_computation.7 | async-start | bytes 4587520 | tf_op jit(solution)/shard_map/all_gather | solution.py:80
  19.7 213.6 %all-gather.22.cloned.1.call-start = ((), (), s32[]{:S(2)}) async-start(), calls=%async_computation.6 | async-start | bytes 4587520 | tf_op jit(solution)/shard_map/all_gather | solution.py:76
  20.5 315.4 %all-reduce.3.cloned.1.call-start = ((), (), s32[]{:S(2)}) async-start(), calls=%async_computation.8 | async-start | bytes 3670016 | tf_op jit(solution)/shard_map/psum | solution.py:115
  239.9 97.8 %copy-start.4 = (f32[3584]{0:T(1024)S(1)}, f32[3584]{0:T(1024)}, u32[]{:S(2)}) copy-start(f32[3584]{0:T(1024)} %param.31) | copy-start | bytes 43012
  239.9 99.9 %copy-start.5 = (f32[3584]{0:T(1024)S(1)}, f32[3584]{0:T(1024)}, u32[]{:S(2)}) copy-start(f32[3584]{0:T(1024)} %param.32) | copy-start | bytes 43012
  239.9 132.5 %all-gather.26.cloned.1.call-start = ((), (), s32[]{:S(2)}) async-start(), calls=%async_computation.9 | async-start | bytes 4587520 | tf_op jit(solution)/shard_map/all_gather | solution.py:118
  335.9 3.9 copy-start
  337.8 3.5 copy-start.6
  341.3 93.4 %copy-start.7 = (s32[128]{0:T(128)S(1)}, s32[128]{0:T(128)}, u32[]{:S(2)}) copy-start(s32[128]{0:T(128)} %param.19) | copy-start | bytes 1540
Sparse Core Ops, SparseCore 0:
  9.5 23.8 all-gather.13
  35.0 21.0 all-gather.15
  57.7 31.4 all-gather.19
  90.6 31.4 all-gather.17
  123.5 21.0 all-gather.9
  146.1 21.0 all-gather.11
  168.7 31.4 all-gather.23
  201.8 31.4 all-gather.21
  240.1 95.7 all-reduce.2
  341.4 30.9 all-gather.25
where the time goes:
time: 452 us
  waiting for transfers between devices  324 us (72%)
  blocking collectives  45.9 us (10%)
  matrix products  42.5 us (9%)
  other arithmetic  17.5 us (4%)
  between operations  16.3 us (4%)
  local copies, waits for them, and re-layouts  5.26 us (1%)
    psum x1, waiting for transfers between devices, on_device(): attended = lax.psum(partial_value, 'tensor')  95.7 us
    psum x1, blocking collectives, on_device(): summed_terms = lax.psum(vocab_sums, ('cand', 'tensor'))  39.3 us
    all_gather x1, waiting for transfers between devices, on_device(): lax.all_gather(base_o, 'cand', axis=1, tiled=True)  33.1 us
    all_gather x1, waiting for transfers between devices, on_device(): lax.all_gather(base_q, 'cand', axis=0, tiled=True)  32.9 us
    all_gather x1, waiting for transfers between devices, on_device(): lax.all_gather(final_rows, 'cand', axis=0, tiled=True)  31.1 us
    all_gather x1, waiting for transfers between devices, on_device(): lax.all_gather(summed[0], 'cand', axis=0, tiled=True)  29.2 us
    all_gather x1, waiting for transfers between devices, on_device(): lax.all_gather(summed[3], 'cand', axis=1, tiled=True)  29.1 us
    dot_general x1, matrix products, on_device(): jnp.dot(lax.all_gather(final_rows, 'cand', axis=0, tiled=True), unembed,...  22.9 us
  transfers between devices with their start and end apart: 10, of which 10 were waited for; matrix products, arithmetic and copies ran while one was open for 6% of the time, Pallas kernels for 0%

commit v1 on v0

--- a/solution.py
+++ b/solution.py
@@ -125,7 +125,7 @@
     matches = local_ids[:, None] == vocab_index[None, :]
     picked = jnp.sum(jnp.where(matches, capped, 0.0), axis=1)
     vocab_sums = jnp.stack([totals, picked], axis=0)
-    summed_terms = lax.psum(vocab_sums, ("cand", "tensor"))
+    summed_terms = lax.psum(lax.psum(vocab_sums, "tensor"), "cand")
     own_terms = lax.dynamic_slice_in_dim(summed_terms, cand_id * length, length, 1)
     mask_values = loss_mask.astype(jnp.float32)
     token_loss = mask_values * (jnp.log(own_terms[0]) - own_terms[1])

time: 452 us -> 439 us (0.971)
  blocking collectives: 45.9 us -> 33.1 us
    psum x1 -> x2, blocking collectives: 39.3 us -> 27.3 us  [on_device(): summed_terms = lax.psum(lax.psum(vocab_sums, 'tensor'), 'cand')]
where the time goes in v1:
time: 439 us
  waiting for transfers between devices  324 us (74%)
  matrix products  42.5 us (10%)
  blocking collectives  33.1 us (8%)
  other arithmetic  17.6 us (4%)
  between operations  16.3 us (4%)
  local copies, waits for them, and re-layouts  5.25 us (1%)
    psum x1, waiting for transfers between devices, on_device(): attended = lax.psum(partial_value, 'tensor')  95.7 us
    all_gather x1, waiting for transfers between devices, on_device(): lax.all_gather(base_o, 'cand', axis=1, tiled=True)  33.1 us
    all_gather x1, waiting for transfers between devices, on_device(): lax.all_gather(base_q, 'cand', axis=0, tiled=True)  32.9 us
    all_gather x1, waiting for transfers between devices, on_device(): lax.all_gather(final_rows, 'cand', axis=0, tiled=True)  31.1 us
    all_gather x1, waiting for transfers between devices, on_device(): lax.all_gather(summed[0], 'cand', axis=0, tiled=True)  29.2 us
    all_gather x1, waiting for transfers between devices, on_device(): lax.all_gather(summed[3], 'cand', axis=1, tiled=True)  29.1 us
    psum x2, blocking collectives, on_device(): summed_terms = lax.psum(lax.psum(vocab_sums, 'tensor'), 'cand')  27.3 us
    dot_general x1, matrix products, on_device(): jnp.dot(lax.all_gather(final_rows, 'cand', axis=0, tiled=True), unembed,...  22.9 us
  transfers between devices with their start and end apart: 10, of which 10 were waited for; matrix products, arithmetic and copies ran while one was open for 6% of the time, Pallas kernels for 0%

profile of v1, /device:TPU:0, one launch (start us, length us, event | category | flops | bytes accessed | tf_op | source)
XLA Modules:
  0.0 438.9 jit_solution(14010259344181664347)
XLA Ops:
  7.2 0.0 copy-start.2
  7.2 0.0 all-gather.14.cloned.1.call-start
  7.2 1.9 constant_dynamic-slice_fusion.1
  9.2 0.0 all-gather.14.cloned.1.call-update
  9.2 0.0 all-gather.16.cloned.1.call-start
  9.2 2.3 dynamic-slice_reduce_fusion
  11.5 0.0 all-gather.16.cloned.1.call-update
  11.5 0.0 all-gather.20.cloned.1.call-start
  11.6 1.5 reduce_sum.123
  13.1 0.0 all-gather.20.cloned.1.call-update
  13.2 0.0 all-gather.18.cloned.1.call-start
  13.2 0.5 all-gather.18.cloned.1.call-update
  13.7 0.0 all-gather.10.cloned.1.call-start
  13.8 1.8 constant_dynamic-slice_fusion.2
  15.6 0.0 all-gather.10.cloned.1.call-update
  15.6 0.0 copy-start.8
  15.7 0.0 all-gather.12.cloned.1.call-start
  15.7 2.4 dynamic-slice_reduce_fusion.1
  18.1 0.0 all-gather.12.cloned.1.call-update
  18.1 0.0 all-gather.24.cloned.1.call-start
  18.2 0.0 copy-done.3
  18.2 1.5 reduce_sum.125
  19.7 0.0 all-gather.24.cloned.1.call-update
  19.7 0.0 all-gather.22.cloned.1.call-start
  19.8 0.7 all-gather.22.cloned.1.call-update
  20.5 0.0 all-reduce.3.cloned.1.call-start
  20.5 0.6 dynamic_slice.22
  23.1 0.6 dynamic_slice.23
  23.7 0.0 copy-done.1
  23.7 0.3 fusion.4
  24.0 0.3 multiply_cosine_fusion
  24.3 9.1 %all-gather.14.cloned.1.call-done = bf16[3584,256]{1,0:T(8,128)(2,1)} async-done(((bf16[896,256]{1,0:T(8,128)(2,1)}), bf16[3584,256]{1,0:T(8,128)(2,1)}) %all-gather.14.cloned.1.call-update) | async-done | bytes 1835024 | tf_op jit(solution)/shard_map/all_gather | solution.py:74
  33.4 22.7 %all-gather.16.cloned.1.call-done = bf16[3584,256]{1,0:T(8,128)(2,1)} async-done(((bf16[896,256]{1,0:T(8,128)(2,1)}), bf16[3584,256]{1,0:T(8,128)(2,1)}) %all-gather.16.cloned.1.call-update) | async-done | bytes 1835024 | tf_op jit(solution)/shard_map/all_gather | solution.py:78
  56.1 3.6 fusion.20
  59.7 0.3 fusion.37
  60.0 29.2 %all-gather.20.cloned.1.call-done = bf16[3584,512]{1,0:T(8,128)(2,1)} async-done(((bf16[896,512]{1,0:T(8,128)(2,1)}), bf16[3584,512]{1,0:T(8,128)(2,1)}) %all-gather.20.cloned.1.call-update) | async-done | bytes 3670032 | tf_op jit(solution)/shard_map/all_gather | solution.py:77
  89.2 32.9 %all-gather.18.cloned.1.call-done = bf16[3584,512]{1,0:T(8,128)(2,1)} async-done(((bf16[896,512]{1,0:T(8,128)(2,1)}), bf16[3584,512]{1,0:T(8,128)(2,1)}) %all-gather.18.cloned.1.call-update) | async-done | bytes 3670032 | tf_op jit(solution)/shard_map/all_gather | solution.py:73
  122.1 5.2 %fusion = f32[128,512]{1,0:T(8,128)S(1)} fusion(bf16[3584,512]{1,0:T(8,128)(2,1)} %all-gather.20.cloned.1.call-done, bf16[3584,512]{1,0:T(8,128)(2,1)} %all-gather.18.cloned.1.call-done, f32[]{:T(128)} %bitcast.1, bf16[128,3584]{1,0:T(8,128)(2,1)S(1)} %copy-done.1, f32[3584]{0:T(1024)S(1)} %copy-done.8, f32[128]{0:T(128)S(1)} %add_rsqrt_fusion.2), kind=kOutput, calls=%fused_computation.6 | convolution fusion | flops 480772096 | bytes 8534532 | tf_op jit(solution)/shard_map/dot_general | solution.py:91
  127.3 0.2 reshape.177
  127.5 0.1 fusion.53
  127.7 0.2 fusion.15
  127.9 16.7 %all-gather.10.cloned.1.call-done = bf16[3584,256]{1,0:T(8,128)(2,1)} async-done(((bf16[896,256]{1,0:T(8,128)(2,1)}), bf16[3584,256]{1,0:T(8,128)(2,1)}) %all-gather.10.cloned.1.call-update) | async-done | bytes 1835024 | tf_op jit(solution)/shard_map/all_gather | solution.py:75
  144.6 22.5 %all-gather.12.cloned.1.call-done = bf16[3584,256]{1,0:T(8,128)(2,1)} async-done(((bf16[896,256]{1,0:T(8,128)(2,1)}), bf16[3584,256]{1,0:T(8,128)(2,1)}) %all-gather.12.cloned.1.call-update) | async-done | bytes 1835024 | tf_op jit(solution)/shard_map/all_gather | solution.py:79
  167.2 3.9 convolution_convert_fusion
  171.1 29.1 %all-gather.24.cloned.1.call-done = bf16[512,3584]{1,0:T(8,128)(2,1)} async-done(((bf16[512,896]{1,0:T(8,128)(2,1)}), bf16[512,3584]{1,0:T(8,128)(2,1)}) %all-gather.24.cloned.1.call-update) | async-done | bytes 3670032 | tf_op jit(solution)/shard_map/all_gather | solution.py:80
  200.2 33.1 %all-gather.22.cloned.1.call-done = bf16[512,3584]{1,0:T(8,128)(2,1)} async-done(((bf16[512,896]{1,0:T(8,128)(2,1)}), bf16[512,3584]{1,0:T(8,128)(2,1)}) %all-gather.22.cloned.1.call-update) | async-done | bytes 3670032 | tf_op jit(solution)/shard_map/all_gather | solution.py:76
  233.3 6.6 %fusion.1 = f32[128,3584]{1,0:T(8,128)} fusion(bf16[128,512]{0,1:T(8,128)(2,1)S(1)} %bitcast.38, bf16[512,3584]{1,0:T(8,128)(2,1)} %all-gather.24.cloned.1.call-done, bf16[512,3584]{1,0:T(8,128)(2,1)} %all-gather.22.cloned.1.call-done, f32[]{:T(128)} %bitcast.1), kind=kOutput, calls=%fused_computation.7 | convolution fusion | flops 478937088 | bytes 9306116 | tf_op jit(solution)/shard_map/dot_general | solution.py:111
  239.9 0.0 all-reduce.3.cloned.1.call-update
  239.9 0.2 all-gather.26.cloned.1.call-start
  240.2 95.7 %all-reduce.3.cloned.1.call-done = f32[128,3584]{1,0:T(8,128)} async-done(((f32[128,3584]{1,0:T(8,128)}), f32[128,3584]{1,0:T(8,128)}) %all-reduce.3.cloned.1.call-update) | async-done | bytes 1835024 | tf_op jit(solution)/shard_map/psum | solution.py:115
  335.9 1.8 multiply_reduce_fusion.1
  337.8 0.0 copy-start.6
  337.8 2.0 multiply_reduce_fusion
  339.8 1.4 multiply_convert_fusion
  341.2 0.0 all-gather.26.cloned.1.call-update
  341.3 0.0 copy-start.7
  341.3 31.1 %all-gather.26.cloned.1.call-done = bf16[512,3584]{1,0:T(8,128)(2,1)} async-done(((bf16[128,3584]{1,0:T(8,128)(2,1)}), bf16[512,3584]{1,0:T(8,128)(2,1)}) %all-gather.26.cloned.1.call-update) | async-done | bytes 3670032 | tf_op jit(solution)/shard_map/all_gather | solution.py:118
  372.4 22.9 %exponential_reduce_fusion = (f32[512]{0:T(512)S(1)}, f32[512]{0:T(512)S(1)}) fusion(s32[512]{0:T(512)S(1)} %broadcast_subtract_fusion, bf16[512,3584]{1,0:T(8,128)(2,1)} %all-gather.26.cloned.1.call-done, bf16[3584,4096]{1,0:T(8,128)(2,1)} %param.33), kind=kOutput, calls=%fused_computation.2 | convolution fusion | flops 15044968448 | bytes 33036288 | tf_op jit(solution)/shard_map/dot_general | solution.py:117
  395.3 21.4 %psum.36 = f32[2,512]{1,0:T(2,128)S(1)} all-reduce(f32[2,512]{1,0:T(2,128)S(1)} %pad_maximum_fusion), channel_id=1, replica_groups=mesh['cand'=4,'tensor'=8] {'tensor'}, use_global_device_ids=true, to_apply=%region_11.12 | all-reduce | flops 1024 | bytes 8192 | tf_op jit(solution)/shard_map/psum | solution.py:128
  416.7 5.9 %psum.37 = f32[2,512]{1,0:T(2,128)S(1)} all-reduce(f32[2,512]{1,0:T(2,128)S(1)} %psum.36), channel_id=1, replica_groups=mesh['cand'=4,'tensor'=8] {'cand'}, use_global_device_ids=true, to_apply=%region_12.13 | all-reduce | flops 1024 | bytes 8192 | tf_op jit(solution)/shard_map/psum | solution.py:128
  422.6 1.2 fusion.52
  423.8 1.9 compare_select_fusion
  425.7 5.8 %all-reduce = (f32[4]{0:T(128)S(1)}, f32[4]{0:T(128)S(1)}) all-reduce(f32[4]{0:T(128)S(1)} %get-tuple-element.18, f32[4]{0:T(128)S(1)} %get-tuple-element.17), channel_id=1, replica_groups=mesh['cand'=4,'tensor'=8] {'cand'}, use_global_device_ids=true, to_apply=%region_14.15 | all-reduce | flops 8 | bytes 64 | tf_op jit(solution)/shard_map/psum | solution.py:133
  431.5 0.5 maximum_divide_fusion
  (26 shorter events, 0.1 us)
Async XLA Ops:
  7.2 4.4 %copy-start.2 = (bf16[2,896,512]{2,1,0:T(8,128)(2,1)S(1)}, bf16[2,896,512]{2,1,0:T(8,128)(2,1)}, u32[]{:S(2)}) copy-start(bf16[2,896,512]{2,1,0:T(8,128)(2,1)} %param.23) | copy-start | bytes 5505028
  7.2 26.2 %all-gather.14.cloned.1.call-start = ((), (), s32[]{:S(2)}) async-start(), calls=%async_computation.2 | async-start | bytes 2293760 | tf_op jit(solution)/shard_map/all_gather | solution.py:74
  9.2 46.9 %all-gather.16.cloned.1.call-start = ((), (), s32[]{:S(2)}) async-start(), calls=%async_computation.3 | async-start | bytes 2293760 | tf_op jit(solution)/shard_map/all_gather | solution.py:78
  11.5 77.6 %all-gather.20.cloned.1.call-start = ((), (), s32[]{:S(2)}) async-start(), calls=%async_computation.5 | async-start | bytes 4587520 | tf_op jit(solution)/shard_map/all_gather | solution.py:77
  13.1 5.0 %copy-start.3 = (bf16[2,512,896]{2,1,0:T(8,128)(2,1)S(1)}, bf16[2,512,896]{2,1,0:T(8,128)(2,1)}, u32[]{:S(2)}) copy-start(bf16[2,512,896]{2,1,0:T(8,128)(2,1)} %param.29) | copy-start | bytes 5505028
  13.2 108.9 %all-gather.18.cloned.1.call-start = ((), (), s32[]{:S(2)}) async-start(), calls=%async_computation.4 | async-start | bytes 4587520 | tf_op jit(solution)/shard_map/all_gather | solution.py:73
  13.7 130.9 %all-gather.10.cloned.1.call-start = ((), (), s32[]{:S(2)}) async-start(), calls=%async_computation | async-start | bytes 2293760 | tf_op jit(solution)/shard_map/all_gather | solution.py:75
  15.6 4.9 %copy-start.9 = (s32[4]{0:T(128)S(1)}, s32[4]{0:T(128)}, u32[]{:S(2)}) copy-start(s32[4]{0:T(128)} %param.20) | copy-start | bytes 52
  15.6 7.4 %copy-start.10 = (f32[4]{0:T(128)S(1)}, f32[4]{0:T(128)}, u32[]{:S(2)}) copy-start(f32[4]{0:T(128)} %param.21) | copy-start | bytes 52
  15.6 8.1 %copy-start.1 = (bf16[128,3584]{1,0:T(8,128)(2,1)S(1)}, bf16[128,3584]{1,0:T(8,128)(2,1)}, u32[]{:S(2)}) copy-start(bf16[128,3584]{1,0:T(8,128)(2,1)} %param.17) | copy-start | bytes 2752516
  15.6 40.5 %copy-start.8 = (f32[3584]{0:T(1024)S(1)}, f32[3584]{0:T(1024)}, u32[]{:S(2)}) copy-start(f32[3584]{0:T(1024)} %param.30) | copy-start | bytes 43012
  15.7 151.5 %all-gather.12.cloned.1.call-start = ((), (), s32[]{:S(2)}) async-start(), calls=%async_computation.1 | async-start | bytes 2293760 | tf_op jit(solution)/shard_map/all_gather | solution.py:79
  18.1 182.1 %all-gather.24.cloned.1.call-start = ((), (), s32[]{:S(2)}) async-start(), calls=%async_computation.7 | async-start | bytes 4587520 | tf_op jit(solution)/shard_map/all_gather | solution.py:80
  19.7 213.6 %all-gather.22.cloned.1.call-start = ((), (), s32[]{:S(2)}) async-start(), calls=%async_computation.6 | async-start | bytes 4587520 | tf_op jit(solution)/shard_map/all_gather | solution.py:76
  20.5 315.4 %all-reduce.3.cloned.1.call-start = ((), (), s32[]{:S(2)}) async-start(), calls=%async_computation.8 | async-start | bytes 3670016 | tf_op jit(solution)/shard_map/psum | solution.py:115
  239.9 97.8 %copy-start.4 = (f32[3584]{0:T(1024)S(1)}, f32[3584]{0:T(1024)}, u32[]{:S(2)}) copy-start(f32[3584]{0:T(1024)} %param.31) | copy-start | bytes 43012
  239.9 99.9 %copy-start.5 = (f32[3584]{0:T(1024)S(1)}, f32[3584]{0:T(1024)}, u32[]{:S(2)}) copy-start(f32[3584]{0:T(1024)} %param.32) | copy-start | bytes 43012
  239.9 132.5 %all-gather.26.cloned.1.call-start = ((), (), s32[]{:S(2)}) async-start(), calls=%async_computation.9 | async-start | bytes 4587520 | tf_op jit(solution)/shard_map/all_gather | solution.py:118
  335.9 3.9 copy-start
  337.8 3.5 copy-start.6
  341.3 81.4 %copy-start.7 = (s32[128]{0:T(128)S(1)}, s32[128]{0:T(128)}, u32[]{:S(2)}) copy-start(s32[128]{0:T(128)} %param.19) | copy-start | bytes 1540
Sparse Core Ops, SparseCore 0:
  9.5 23.8 all-gather.13
  35.0 21.0 all-gather.15
  57.7 31.4 all-gather.19
  90.6 31.4 all-gather.17
  123.5 21.0 all-gather.9
  146.1 21.0 all-gather.11
  168.7 31.4 all-gather.23
  201.8 31.4 all-gather.21
  240.1 95.7 all-reduce.2
  341.4 30.9 all-gather.25
